TPU v7x, 32 devices: a whole 2x2x4 slice. The times are simulated.
32 devices in a mesh: cuts: 2 (over x), wide: 8 (over z, y), narrow: 2 (over core).
Axes of the slice: x: 2, y: 2, z: 4, core: 2. Of those that a mesh axis runs over, the one named last changes fastest.
Arguments:
- stem_tensor: float32 [2, 16384, 512], P(None, ('cuts', 'wide', 'narrow')), parts along dimension 1, may hold values from -6 to 6
- leaves: bfloat16 [16, 4, 2, 512, 512], P(('cuts', 'wide')), parts along dimension 0, may hold values from -1 to 1
- root_devices: int32 [4], replicated, may hold values from 0 to 7, as said below
- mode_orders: int32 [4, 9], replicated, may hold values from 0 to 8, each once within a row
Outputs:
- contracted: float32 [2, 16384, 512], P(None, ('cuts', 'wide', 'narrow')), parts along dimension 1
There are 2 independent parts, one for each index of `cuts`. A program takes and returns all parts, laid end to end along the dimension named above; an argument that names none is the same for every part. Nothing has to cross between parts.
Inputs may be any that keep to these rules, and one draw needn't show every extreme that they name: `root_devices`: the roots include 0, 4 and 7. `mode_orders`: each row holds every number of 0 to 8 once.
All inputs are finite; a program needn't handle non-finite values.
Results may differ from a plain program's by a relative error of at most 0.0081.
Values may be sent and summed in bfloat16 or wider, within the bound.
A program may use at most 64 MiB of HBM per device.

v0:
```python
import jax
import jax.numpy as jnp
from jax import lax
from jax.sharding import PartitionSpec as P

STEPS = 4


def from_partner(value, axis, apart):
    return lax.ppermute(value, axis, [(i, i ^ 1 << apart) for i in range(lax.axis_size(axis))])


def broadcast(block, axis, holder):
    block = jnp.where(lax.axis_index(axis) == holder, block, jnp.zeros_like(block))
    return lax.psum(block, axis)


def complex_product(left_matrix, right_matrix, precision=None):
    real_part = jnp.dot(
        left_matrix[0], right_matrix[0], preferred_element_type=jnp.float32, precision=precision
    ) - jnp.dot(
        left_matrix[1], right_matrix[1], preferred_element_type=jnp.float32, precision=precision
    )
    imag_part = jnp.dot(
        left_matrix[0], right_matrix[1], preferred_element_type=jnp.float32, precision=precision
    ) + jnp.dot(
        left_matrix[1], right_matrix[0], preferred_element_type=jnp.float32, precision=precision
    )
    return jnp.stack([real_part, imag_part])


def column_source(order_row, branch_width):
    column = jnp.arange(branch_width, dtype=jnp.int32)
    mode_count = order_row.shape[0]
    powers = jnp.left_shift(jnp.int32(1), jnp.arange(mode_count, dtype=jnp.int32))
    bit_table = column[:, None] // powers[None, :] % 2
    weights = jnp.left_shift(jnp.int32(1), order_row)
    return jnp.sum(bit_table * weights[None, :], axis=1)


def stem_product(network, ordered):
    highest = lax.Precision.HIGHEST
    return complex_product(network, ordered, highest)


def local(stem_tensor, leaves, root_devices, mode_orders):
    network = stem_tensor
    branch_width = stem_tensor.shape[2]
    rows_local = stem_tensor.shape[1]
    core_count = lax.axis_size("narrow")
    row_share = branch_width // core_count
    core_index = lax.axis_index("narrow")
    wide_index = lax.axis_index("wide")
    lower_leaf = wide_index % 2 == 0
    lower_pair = wide_index // 2 % 2 == 0
    for step_index in range(STEPS):
        own_leaf = leaves[0, step_index]
        partner = from_partner(own_leaf, "wide", 0)
        left_leaf = jnp.where(lower_leaf, own_leaf, partner)
        right_leaf = jnp.where(lower_leaf, partner, own_leaf)
        source = column_source(mode_orders[step_index], branch_width)
        row_block = lax.dynamic_slice_in_dim(left_leaf, core_index * row_share, row_share, 1)
        pair_part = complex_product(row_block, right_leaf).astype(jnp.bfloat16)
        pair_other = from_partner(pair_part, "wide", 1)
        pair_lower = jnp.where(lower_pair, pair_part, pair_other)
        pair_upper = jnp.where(lower_pair, pair_other, pair_part)
        branch_part = complex_product(
            pair_lower, lax.all_gather(pair_upper, "narrow", axis=1, tiled=True)
        )
        ordered_part = jnp.take(branch_part, source, axis=2)
        ordered_part = broadcast(ordered_part, "wide", root_devices[step_index])
        current = network
        network = stem_product(current, lax.all_gather(ordered_part, "narrow", axis=1, tiled=True))
        if step_index % 2 == 0:
            stem_view = network.reshape(2, rows_local, core_count, row_share)
            network = lax.all_to_all(
                stem_view, "narrow", split_axis=2, concat_axis=2, tiled=True
            ).reshape(2, rows_local, branch_width)
    return network


def solution(mesh):
    placed = (
        P(None, ("cuts", "wide", "narrow"), None),
        P(("cuts", "wide"), None, None, None, None),
        P(),
        P(),
    )
    return jax.shard_map(
        local,
        mesh=mesh,
        in_specs=placed,
        out_specs=P(None, ("cuts", "wide", "narrow"), None),
        check_vma=False,
    )
```

profile of v0, /device:TPU:0, one launch (start us, length us, event | category | flops | bytes accessed | tf_op | source)
XLA Modules:
  0.0 470.5 jit_solution(2376073138795786767)
XLA Ops:
  6.5 4.3 slice_bitcast_fusion
  19.7 85.0 %collective-permute-done.4 = bf16[2,512,512]{2,1,0:T(8,128)(2,1)S(1)} collective-permute-done((bf16[2,512,512]{2,1,0:T(8,128)(2,1)}, bf16[2,512,512]{2,1,0:T(8,128)(2,1)S(1)}, u32[]{:S(2)}, u32[]{:S(2)}) %collective-permute-start.4) | collective-permute-done | bytes 1048608 | tf_op jit(solution)/shard_map/ppermute | solution.py:10
  108.2 3.8 broadcast_select_fusion.3
  120.7 9.9 %collective-permute-done.3 = bf16[2,256,512]{2,1,0:T(8,128)(2,1)S(1)} collective-permute-done((bf16[2,256,512]{2,1,0:T(8,128)(2,1)S(1)}, bf16[2,256,512]{2,1,0:T(8,128)(2,1)S(1)}, u32[]{:S(2)}, u32[]{:S(2)}) %collective-permute-start.3) | collective-permute-done | bytes 524320 | tf_op jit(solution)/shard_map/ppermute | solution.py:10
  135.5 6.4 %collective-permute-done.5 = bf16[2,256,512]{2,1,0:T(8,128)(2,1)} collective-permute-done((bf16[2,256,512]{2,1,0:T(8,128)(2,1)}, bf16[2,256,512]{2,1,0:T(8,128)(2,1)}, u32[]{:S(2)}, u32[]{:S(2)}) %collective-permute-start.5) | collective-permute-done | bytes 524320 | tf_op jit(solution)/shard_map/ppermute | solution.py:10
  147.0 4.5 collective-permute-done.1
  156.5 10.7 %collective-permute-done.7 = bf16[2,256,512]{2,1,0:T(8,128)(2,1)S(1)} collective-permute-done((bf16[2,256,512]{2,1,0:T(8,128)(2,1)S(1)}, bf16[2,256,512]{2,1,0:T(8,128)(2,1)S(1)}, u32[]{:S(2)}, u32[]{:S(2)}) %collective-permute-start.7) | collective-permute-done | bytes 524320 | tf_op jit(solution)/shard_map/ppermute | solution.py:10
  204.7 3.6 bitcast_select_fusion.2
  216.3 156.5 %all-reduce.3.cloned.1.call-done = (f32[2,256,512]{1,0,2:T(2,128)}, f32[2,256,512]{1,0,2:T(2,128)}, f32[2,256,512]{1,0,2:T(2,128)}, f32[2,256,512]{1,0,2:T(2,128)}) async-done(((f32[2,256,512]{1,0,2:T(2,128)}, f32[2,256,512]{1,0,2:T(2,128)}, f32[2,256,512]{1,0,2:T(2,128)}, f32[2,256,512]{1,0,2:T(2,128)}), (f32[2,256,512]{1,0,2:T(2,128)}, f32[2,256,512]{1,0,2:T(2,128)}, f32[2,256,512]{1,0,2:T(2,128)}, ...) | async-done | bytes 4194320 | tf_op jit(solution)/shard_map/psum | solution.py:15
  375.0 8.3 %all-gather.11.cloned.1.call-done = f32[2,512,512]{1,0,2:T(2,128)} async-done(((f32[2,256,512]{1,0,2:T(2,128)}), f32[2,512,512]{1,0,2:T(2,128)}) %all-gather.11.cloned.1.call-update) | async-done | bytes 2097168 | tf_op jit(solution)/shard_map/all_gather | solution.py:73
  383.3 4.0 fusion.99
  396.4 5.0 %all-to-all-start = ((f32[2,512,2,256]{1,3,0,2:T(8,128)}), f32[2,512,2,256]{1,3,0,2:T(8,128)}, u32[]{:S(2)}, u32[]{:S(2)}) async-start(f32[2,512,2,256]{1,3,0,2:T(8,128)} %pad_maximum_fusion), calls=%async_computation | async-start | bytes 4194304 | tf_op jit(solution)/shard_map/all_to_all | solution.py:76
  401.5 4.0 fusion.97
  408.5 4.5 fusion.38
  413.0 4.0 fusion.96
  417.1 3.5 fusion.42
  420.5 3.9 convolution_subtract_fusion.2
  428.3 3.5 convolution_add_fusion.2
  437.2 4.8 %all-to-all-start.1 = ((f32[2,512,2,256]{1,3,0,2:T(8,128)}), f32[2,512,2,256]{1,3,0,2:T(8,128)}, u32[]{:S(2)}, u32[]{:S(2)}) async-start(f32[2,512,2,256]{1,3,0,2:T(8,128)} %pad_maximum_fusion.1), calls=%async_computation.1 | async-start | bytes 4194304 | tf_op jit(solution)/shard_map/all_to_all | solution.py:76
  442.0 4.0 fusion.94
  447.9 3.6 fusion.26
  451.4 3.6 fusion.30
  455.0 3.7 fusion
  458.7 3.6 fusion.1
  (176 shorter events, 105.2 us)
Async XLA Ops:
  6.5 9.4 %copy-start.24 = (s32[4,9]{1,0:T(4,128)S(1)}, s32[4,9]{1,0:T(4,128)}, u32[]{:S(2)}) copy-start(s32[4,9]{1,0:T(4,128)} %param.11) | copy-start | bytes 436
  6.5 9.9 %copy-start.23 = (s32[4]{0:T(128)S(1)}, s32[4]{0:T(128)}, u32[]{:S(2)}) copy-start(s32[4]{0:T(128)} %param.10) | copy-start | bytes 52
  6.5 162.2 %all-gather.13.cloned.1.call-start = ((), (), s32[]{:S(2)}) async-start(), calls=%async_computation.4 | async-start | bytes 1572864 | tf_op jit(solution)/shard_map/all_gather | solution.py:68
  10.9 95.3 %collective-permute-start.6 = (bf16[2,512,512]{2,1,0:T(8,128)(2,1)}, bf16[2,512,512]{2,1,0:T(8,128)(2,1)S(1)}, u32[]{:S(2)}, u32[]{:S(2)}) collective-permute-start(bf16[2,512,512]{2,1,0:T(8,128)(2,1)} %get-tuple-element.19), channel_id=1, source_target_pairs={{0,2},{2,0},{4,6},{6,4},{8,10},{10,8},{12,14},{14,12},{1,3},{3,1},... | collective-permute-start | bytes 3145736 | tf_op jit(solution)/shard_map/ppermute | solution.py:10
  13.9 92.3 %collective-permute-start.2 = (bf16[2,512,512]{2,1,0:T(8,128)(2,1)}, bf16[2,512,512]{2,1,0:T(8,128)(2,1)S(1)}, u32[]{:S(2)}, u32[]{:S(2)}) collective-permute-start(bf16[2,512,512]{2,1,0:T(8,128)(2,1)} %get-tuple-element.20), channel_id=1, source_target_pairs={{0,2},{2,0},{4,6},{6,4},{8,10},{10,8},{12,14},{14,12},{1,3},{3,1},... | collective-permute-start | bytes 3145736 | tf_op jit(solution)/shard_map/ppermute | solution.py:10
  13.9 94.3 %collective-permute-start = (bf16[2,512,512]{2,1,0:T(8,128)(2,1)}, bf16[2,512,512]{2,1,0:T(8,128)(2,1)}, u32[]{:S(2)}, u32[]{:S(2)}) collective-permute-start(bf16[2,512,512]{2,1,0:T(8,128)(2,1)} %get-tuple-element.21), channel_id=1, source_target_pairs={{0,2},{2,0},{4,6},{6,4},{8,10},{10,8},{12,14},{14,12},{1,3},{3,1},... | collective-permute-start | bytes 3145736 | tf_op jit(solution)/shard_map/ppermute | solution.py:10
  15.9 88.8 %collective-permute-start.4 = (bf16[2,512,512]{2,1,0:T(8,128)(2,1)}, bf16[2,512,512]{2,1,0:T(8,128)(2,1)S(1)}, u32[]{:S(2)}, u32[]{:S(2)}) collective-permute-start(bf16[2,512,512]{2,1,0:T(8,128)(2,1)} %get-tuple-element.22), channel_id=1, source_target_pairs={{0,2},{2,0},{4,6},{6,4},{8,10},{10,8},{12,14},{14,12},{1,3},{3,1},... | collective-permute-start | bytes 3145736 | tf_op jit(solution)/shard_map/ppermute | solution.py:10
  115.7 14.9 %collective-permute-start.3 = (bf16[2,256,512]{2,1,0:T(8,128)(2,1)S(1)}, bf16[2,256,512]{2,1,0:T(8,128)(2,1)S(1)}, u32[]{:S(2)}, u32[]{:S(2)}) collective-permute-start(bf16[2,256,512]{2,1,0:T(8,128)(2,1)S(1)} %pad_maximum_fusion.8), channel_id=1, source_target_pairs={{0,4},{2,6},{4,0},{6,2},{8,12},{10,14},{12,8},{14,10},{1,5},{3,7},... | collective-permute-start | bytes 1572872 | tf_op jit(solution)/shard_map/ppermute | solution.py:10
  119.1 22.8 %collective-permute-start.5 = (bf16[2,256,512]{2,1,0:T(8,128)(2,1)}, bf16[2,256,512]{2,1,0:T(8,128)(2,1)}, u32[]{:S(2)}, u32[]{:S(2)}) collective-permute-start(bf16[2,256,512]{2,1,0:T(8,128)(2,1)} %pad_maximum_fusion.9), channel_id=1, source_target_pairs={{0,4},{2,6},{4,0},{6,2},{8,12},{10,14},{12,8},{14,10},{1,5},{3,7},... | collective-permute-start | bytes 1572872 | tf_op jit(solution)/shard_map/ppermute | solution.py:10
  131.5 41.6 %all-gather.17.cloned.1.call-start = ((), (), s32[]{:S(2)}) async-start(), calls=%async_computation.6 | async-start | bytes 1572864 | tf_op jit(solution)/shard_map/all_gather | solution.py:68
  132.2 9.8 %copy-start.18 = (bf16[1,256,512]{2,1,0:T(8,128)(2,1)S(1)}, bf16[1,256,512]{2,1,0:T(8,128)(2,1)}, u32[]{:S(2)}) copy-start(bf16[1,256,512]{2,1,0:T(8,128)(2,1)} %copy-done.17) | copy-start | bytes 786436
  133.7 17.7 %collective-permute-start.1 = (bf16[2,256,512]{2,1,0:T(8,128)(2,1)}, bf16[2,256,512]{2,1,0:T(8,128)(2,1)}, u32[]{:S(2)}, u32[]{:S(2)}) collective-permute-start(bf16[2,256,512]{2,1,0:T(8,128)(2,1)} %pad_maximum_fusion.7), channel_id=1, source_target_pairs={{0,4},{2,6},{4,0},{6,2},{8,12},{10,14},{12,8},{14,10},{1,5},{3,7},... | collective-permute-start | bytes 1572872 | tf_op jit(solution)/shard_map/ppermute | solution.py:10
  143.9 37.9 %all-gather.9.cloned.1.call-start = ((), (), s32[]{:S(2)}) async-start(), calls=%async_computation.2 | async-start | bytes 1572864 | tf_op jit(solution)/shard_map/all_gather | solution.py:68
  153.5 32.4 %all-gather.21.cloned.1.call-start = ((), (), s32[]{:S(2)}) async-start(), calls=%async_computation.8 | async-start | bytes 1572864 | tf_op jit(solution)/shard_map/all_gather | solution.py:68
  154.9 12.3 %collective-permute-start.7 = (bf16[2,256,512]{2,1,0:T(8,128)(2,1)S(1)}, bf16[2,256,512]{2,1,0:T(8,128)(2,1)S(1)}, u32[]{:S(2)}, u32[]{:S(2)}) collective-permute-start(bf16[2,256,512]{2,1,0:T(8,128)(2,1)S(1)} %pad_maximum_fusion.10), channel_id=1, source_target_pairs={{0,4},{2,6},{4,0},{6,2},{8,12},{10,14},{12,8},{14,10},{1,5},{3,7},... | collective-permute-start | bytes 1572872 | tf_op jit(solution)/shard_map/ppermute | solution.py:10
  168.1 204.6 %all-reduce.3.cloned.1.call-start = ((), (), s32[]{:S(2)}) async-start(), calls=%async_computation.10 | async-start | bytes 8388608 | tf_op jit(solution)/shard_map/psum | solution.py:15
  195.8 6.2 %copy-start.8 = (f32[2,256,512]{1,0,2:T(2,128)S(1)}, f32[2,256,512]{1,0,2:T(2,128)}, u32[]{:S(2)}) copy-start(f32[2,256,512]{1,0,2:T(2,128)} %copy.24) | copy-start | bytes 3145732
  216.2 167.1 %all-gather.11.cloned.1.call-start = ((), (), s32[]{:S(2)}) async-start(), calls=%async_computation.3 | async-start | bytes 3145728 | tf_op jit(solution)/shard_map/all_gather | solution.py:73
  372.8 28.7 %all-gather.15.cloned.1.call-start = ((), (), s32[]{:S(2)}) async-start(), calls=%async_computation.5 | async-start | bytes 3145728 | tf_op jit(solution)/shard_map/all_gather | solution.py:73
  373.5 39.5 %all-gather.19.cloned.1.call-start = ((), (), s32[]{:S(2)}) async-start(), calls=%async_computation.7 | async-start | bytes 3145728 | tf_op jit(solution)/shard_map/all_gather | solution.py:73
  374.3 67.8 %all-gather.23.cloned.1.call-start = ((), (), s32[]{:S(2)}) async-start(), calls=%async_computation.9 | async-start | bytes 3145728 | tf_op jit(solution)/shard_map/all_gather | solution.py:73
  375.0 12.3 %copy-start.1 = (f32[2,512,512]{2,1,0:T(8,128)S(1)}, f32[2,512,512]{2,1,0:T(8,128)}, u32[]{:S(2)}) copy-start(f32[2,512,512]{2,1,0:T(8,128)} %param.8) | copy-start | bytes 6291460
  396.4 9.1 %all-to-all-start = ((f32[2,512,2,256]{1,3,0,2:T(8,128)}), f32[2,512,2,256]{1,3,0,2:T(8,128)}, u32[]{:S(2)}, u32[]{:S(2)}) async-start(f32[2,512,2,256]{1,3,0,2:T(8,128)} %pad_maximum_fusion), calls=%async_computation | async-start | bytes 4194304 | tf_op jit(solution)/shard_map/all_to_all | solution.py:76
  437.2 8.9 %all-to-all-start.1 = ((f32[2,512,2,256]{1,3,0,2:T(8,128)}), f32[2,512,2,256]{1,3,0,2:T(8,128)}, u32[]{:S(2)}, u32[]{:S(2)}) async-start(f32[2,512,2,256]{1,3,0,2:T(8,128)} %pad_maximum_fusion.1), calls=%async_computation.1 | async-start | bytes 4194304 | tf_op jit(solution)/shard_map/all_to_all | solution.py:76
  (20 other events, 63.6 us)
Sparse Core Ops, SparseCore 0:
  131.6 9.5 all-gather.12
  144.0 9.5 all-gather.16
  155.1 10.1 all-gather.8
  168.2 8.9 all-gather.20
  216.3 156.3 all-reduce.2
  374.1 9.1 all-gather.10
  384.8 11.2 all-gather.14
  397.7 11.2 all-gather.18
  410.6 11.2 all-gather.22
where the time goes:
time: 476 us; the launch traced here: 471 us
  waiting for transfers between devices  283 us (59%)
  matrix products  65.1 us (14%)
  local copies, waits for them, and re-layouts  47.5 us (10%)
  other arithmetic  36.5 us (8%)
  starting transfers between devices  21.4 us (4%)
  between operations  16.7 us (4%)
    psum x1, waiting for transfers between devices, broadcast(): return lax.psum(block, axis)  156 us
    ppermute x8, waiting for transfers between devices, from_partner(): lax.ppermute(value, axis, [(i, i ^ 1 << apart) for i in range(lax.axis_si...  116 us
    dot_general x12, matrix products, complex_product(): jnp.dot(left_matrix[1], right_matrix[0], preferred_element_type=jnp.float...  17.9 us
    dot_general x12, matrix products, complex_product(): jnp.dot(left_matrix[1], right_matrix[1], preferred_element_type=jnp.float...  17.8 us
    dot_general x12, matrix products, complex_product(): jnp.dot(left_matrix[0], right_matrix[1], preferred_element_type=jnp.float...  15.2 us
    dot_general x12, matrix products, complex_product(): jnp.dot(left_matrix[0], right_matrix[0], preferred_element_type=jnp.float...  14.2 us
    slice x3, local copies, waits for them, and re-layouts, complex_product(): right_matrix[0]  12.1 us
    gather x4, local copies, waits for them, and re-layouts, local(): ordered_part = jnp.take(branch_part, source, axis=2)  11.9 us
  transfers between devices with their start and end apart: 19, of which 7 were waited for; matrix products, arithmetic and copies ran while one was open for 18% of the time, Pallas kernels for 0%

commit v1 on v0

v1 whole, which is shorter than its diff:
```python
import jax
import jax.numpy as jnp
from jax import lax
from jax.sharding import PartitionSpec as P

GROUP = 4


def from_partner(value, axis, mask):
    return lax.ppermute(value, axis, [(i, i ^ mask) for i in range(lax.axis_size(axis))])


def complex_product(a, b):
    def dot(x, y):
        return jnp.dot(x, y, preferred_element_type=jnp.float32)

    real_part = dot(a[0], b[0]) - dot(a[1], b[1])
    imag_part = dot(a[0], b[1]) + dot(a[1], b[0])
    return jnp.stack([real_part, imag_part])


def column_source(order_row, branch_width):
    column = jnp.arange(branch_width, dtype=jnp.int32)
    modes = jnp.arange(order_row.shape[0], dtype=jnp.int32)
    bits = jnp.right_shift(column[:, None], modes[None, :]) & 1
    return jnp.sum(bits * jnp.left_shift(jnp.int32(1), order_row)[None, :], axis=1)


def both_cores(half, axis):
    other = from_partner(half, "narrow", 1)
    core = lax.axis_index("narrow")
    low = jnp.where(core == 0, half, other)
    high = jnp.where(core == 0, other, half)
    return jnp.concatenate([low, high], axis=axis)


def local(stem_tensor, leaves, root_devices, mode_orders):
    width = stem_tensor.shape[2]
    rows = stem_tensor.shape[1]
    half = width // 2
    core = lax.axis_index("narrow")
    wide = lax.axis_index("wide")
    groups = lax.axis_size("wide") // GROUP
    member = wide % GROUP
    y = member % 2
    z = member // 2
    group = wide // GROUP
    bf16 = jnp.bfloat16

    by_parity = leaves[0].reshape(2, 2, 2, width, width)
    mine = lax.dynamic_index_in_dim(by_parity, y, 1, False)
    theirs = lax.dynamic_index_in_dim(by_parity, 1 - y, 1, False)
    sent = lax.dynamic_slice_in_dim(theirs, core * half, half, 2)
    got = both_cores(from_partner(sent, "wide", 1), 2)
    left = jnp.where(y == 0, mine, got)
    right = jnp.where(y == 0, got, mine)
    left = lax.dynamic_slice_in_dim(left, core * half, half, 2)
    pairs = jnp.stack([complex_product(left[i], right[i]).astype(bf16) for i in range(2)])
    own = lax.dynamic_index_in_dim(pairs, z, 0, False)
    away = lax.dynamic_index_in_dim(pairs, 1 - z, 0, False)
    came = from_partner(away, "wide", 2)
    low = jnp.where(z == 0, own, came)
    high = jnp.where(z == 0, came, own)
    source = column_source(lax.dynamic_index_in_dim(mode_orders, member, 0, False), width)
    chosen = (jnp.arange(width, dtype=jnp.int32)[:, None] == source[None, :]).astype(bf16)
    high = jnp.dot(high, chosen, preferred_element_type=jnp.float32).astype(bf16)
    branch = complex_product(low, both_cores(high, 1)).astype(bf16)
    root_group = lax.dynamic_index_in_dim(root_devices, member, 0, False) // GROUP
    step = 1
    while step < groups:
        other = from_partner(branch, "wide", GROUP * step)
        branch = jnp.where((root_group & step) == (group & step), branch, other)
        step *= 2
    first, second = branch[:, : half // 2], branch[:, half // 2 :]
    first_y = from_partner(first, "wide", 1)
    second_z = from_partner(second, "wide", 2)
    pair_y = jnp.stack([first, first_y])
    pair_z = jnp.stack([second, second_z])
    over_z = from_partner(pair_y, "wide", 2)
    over_y = from_partner(pair_z, "wide", 1)
    all_first = jnp.concatenate([pair_y, over_z])
    all_second = jnp.stack([second, over_y[0], second_z, over_y[1]])
    gathered = jnp.concatenate([all_first, all_second], axis=2)
    gathered = both_cores(gathered, 2)

    network = stem_tensor.astype(bf16)
    for k in range(4):
        ordered = lax.dynamic_index_in_dim(gathered, member ^ k, 0, False)
        network = complex_product(network, ordered)
        if k < 3:
            network = network.astype(bf16)
        if k % 2 == 0:
            keep = lax.dynamic_slice_in_dim(network, core * half, half, 2)
            give = lax.dynamic_slice_in_dim(network, (1 - core) * half, half, 2)
            take = from_partner(give, "narrow", 1)
            network = jnp.concatenate(
                [jnp.where(core == 0, keep, take), jnp.where(core == 0, take, keep)], axis=2
            )
    return network


def solution(mesh):
    stem_spec = P(None, ("cuts", "wide", "narrow"), None)
    return jax.shard_map(
        local,
        mesh=mesh,
        in_specs=(stem_spec, P(("cuts", "wide"), None, None, None, None), P(), P()),
        out_specs=stem_spec,
        check_vma=False,
    )
```

time: 476 us -> 123 us (0.26); the launches traced: 471 us -> 123 us
  waiting for transfers between devices: 283 us -> 82 us
  matrix products: 65.1 us -> 11.7 us
  local copies, waits for them, and re-layouts: 47.5 us -> 2.24 us
  other arithmetic: 36.5 us -> 10.3 us
  between operations: 16.7 us -> 2.97 us
  starting transfers between devices: 21.4 us -> 13.5 us
    psum x1 -> x0, waiting for transfers between devices: 156 us -> none  [broadcast(): return lax.psum(block, axis)]
    dot_general x48 -> x29, matrix products: 65.1 us -> 11.7 us  [the longest x28 11.2 us: dot(): return jnp.dot(x, y, preferred_element_type=jnp.float32)]
    ppermute x8 -> x12, waiting for transfers between devices: 116 us -> 82 us  [from_partner(): lax.ppermute(value, axis, [(i, i ^ mask) for i in range(lax.axis_size(axi...]
    select_n x17 -> x9, other arithmetic: 26.4 us -> 4.31 us  [the longest x2 2.09 us: both_cores(): high = jnp.where(core == 0, other, half)]
    slice x7 -> x1, local copies, waits for them, and re-layouts: 21.5 us -> 0.03 us  [local(): all_second = jnp.stack([second, over_y[0], second_z, over_y[1]])]
    gather x4 -> x0, local copies, waits for them, and re-layouts: 11.9 us -> none  [local(): ordered_part = jnp.take(branch_part, source, axis=2)]
    all_to_all x2 -> x0, starting transfers between devices: 9.86 us -> none  [local(): lax.all_to_all(stem_view, 'narrow', split_axis=2, concat_axis=2, tiled=True)]
    all_gather x8 -> x0, waiting for transfers between devices: 8.35 us -> none  [the longest x4 8.31 us: local(): lax.all_gather(ordered_part, 'narrow', axis=1, tiled=True)]
  transfers between devices with their start and end apart: 19 -> 12, of which waited for: 7 -> 11; matrix products, arithmetic and copies ran while one was open for 18% -> 3% of each run, Pallas kernels for 0% -> 0%
where the time goes in v1:
time: 123 us
  waiting for transfers between devices  82 us (67%)
  starting transfers between devices  13.5 us (11%)
  matrix products  11.7 us (10%)
  other arithmetic  10.3 us (8%)
  between operations  2.97 us (2%)
  local copies, waits for them, and re-layouts  2.24 us (2%)
    ppermute x12, waiting for transfers between devices, from_partner(): lax.ppermute(value, axis, [(i, i ^ mask) for i in range(lax.axis_size(axi...  82 us
    ppermute x12, starting transfers between devices, from_partner(): lax.ppermute(value, axis, [(i, i ^ mask) for i in range(lax.axis_size(axi...  13.5 us
    dot_general x28, matrix products, dot(): return jnp.dot(x, y, preferred_element_type=jnp.float32)  11.2 us
  transfers between devices with their start and end apart: 12, of which 11 were waited for; matrix products, arithmetic and copies ran while one was open for 3% of the time, Pallas kernels for 0%

profile of v1, /device:TPU:0, one launch (start us, length us, event | category | flops | bytes accessed | tf_op | source)
XLA Modules:
  0.0 122.7 jit_solution(14624826626916996276)
XLA Ops:
  0.0 1.5 %dynamic-slice_bitcast_fusion.1 = bf16[2,2,256,512]{3,2,1,0:T(8,128)(2,1)S(1)} fusion(bf16[2,2,2,512,512]{4,3,2,1,0:T(8,128)(2,1)} %bitcast.160, s32[]{:T(128)S(6)} %select_n.164, s32[]{:T(128)S(6)} %select_n.166), kind=kLoop, calls=%fused_computation.78 | loop fusion | bytes 2097160 | tf_op jit(solution)/shard_map/dynamic_slice | solution.py:53
  1.5 3.1 %collective-permute-start = (bf16[2,2,256,512]{3,2,1,0:T(8,128)(2,1)S(1)}, bf16[2,2,256,512]{3,2,1,0:T(8,128)(2,1)S(1)}, u32[]{:S(2)}, u32[]{:S(2)}) collective-permute-start(bf16[2,2,256,512]{3,2,1,0:T(8,128)(2,1)S(1)} %dynamic-slice_bitcast_fusion.1), channel_id=1, source_target_pairs={{0,2},{2,0},{4,6},{6,4},{8,10},{10,8},{12,14},{14,12},{1,3},{3,1},... | collective-permute-start | bytes 3145736 | tf_op jit(solution)/shard_map/ppermute | solution.py:10
  4.5 23.1 %collective-permute-done = bf16[2,2,256,512]{3,2,1,0:T(8,128)(2,1)S(1)} collective-permute-done((bf16[2,2,256,512]{3,2,1,0:T(8,128)(2,1)S(1)}, bf16[2,2,256,512]{3,2,1,0:T(8,128)(2,1)S(1)}, u32[]{:S(2)}, u32[]{:S(2)}) %collective-permute-start) | collective-permute-done | bytes 1048608 | tf_op jit(solution)/shard_map/ppermute | solution.py:10
  27.7 2.7 %collective-permute-done.1 = bf16[2,2,256,512]{3,2,1,0:T(8,128)(2,1)S(1)} collective-permute-done((bf16[2,2,256,512]{3,2,1,0:T(8,128)(2,1)S(1)}, bf16[2,2,256,512]{3,2,1,0:T(8,128)(2,1)S(1)}, u32[]{:S(2)}, u32[]{:S(2)}) %collective-permute-start.1) | collective-permute-done | bytes 1048608 | tf_op jit(solution)/shard_map/ppermute | solution.py:10
  30.5 0.8 fusion
  34.6 1.9 %collective-permute-start.2 = (bf16[2,256,512]{2,1,0:T(8,128)(2,1)S(1)}, bf16[2,256,512]{2,1,0:T(8,128)(2,1)S(1)}, u32[]{:S(2)}, u32[]{:S(2)}) collective-permute-start(bf16[2,256,512]{2,1,0:T(8,128)(2,1)S(1)} %dynamic-slice_bitcast_fusion.2), channel_id=1, source_target_pairs={{0,4},{2,6},{4,0},{6,2},{8,12},{10,14},{12,8},{14,10},{1,5},{3,7},... | collective-permute-start | bytes 1572872 | tf_op jit(solution)/shard_map/ppermute | solution.py:10
  37.2 11.5 %collective-permute-done.2 = bf16[2,256,512]{2,1,0:T(8,128)(2,1)S(1)} collective-permute-done((bf16[2,256,512]{2,1,0:T(8,128)(2,1)S(1)}, bf16[2,256,512]{2,1,0:T(8,128)(2,1)S(1)}, u32[]{:S(2)}, u32[]{:S(2)}) %collective-permute-start.2) | collective-permute-done | bytes 524320 | tf_op jit(solution)/shard_map/ppermute | solution.py:10
  49.3 1.8 %collective-permute-done.3 = bf16[2,256,512]{2,1,0:T(8,128)(2,1)S(1)} collective-permute-done((bf16[2,256,512]{2,1,0:T(8,128)(2,1)S(1)}, bf16[2,256,512]{2,1,0:T(8,128)(2,1)S(1)}, u32[]{:S(2)}, u32[]{:S(2)}) %collective-permute-start.3) | collective-permute-done | bytes 524320 | tf_op jit(solution)/shard_map/ppermute | solution.py:10
  52.5 2.8 %collective-permute-start.4 = (bf16[2,256,512]{2,1,0:T(8,128)(2,1)S(1)}, bf16[2,256,512]{2,1,0:T(8,128)(2,1)S(1)}, u32[]{:S(2)}, u32[]{:S(2)}) collective-permute-start(bf16[2,256,512]{2,1,0:T(8,128)(2,1)S(1)} %pad_maximum_fusion.5), channel_id=1, source_target_pairs={{0,8},{2,10},{4,12},{6,14},{8,0},{10,2},{12,4},{14,6},{1,9},{3,11}... | collective-permute-start | bytes 1572872 | tf_op jit(solution)/shard_map/ppermute | solution.py:10
  58.6 20.3 %collective-permute-done.4 = bf16[2,256,512]{2,1,0:T(8,128)(2,1)S(1)} collective-permute-done((bf16[2,256,512]{2,1,0:T(8,128)(2,1)S(1)}, bf16[2,256,512]{2,1,0:T(8,128)(2,1)S(1)}, u32[]{:S(2)}, u32[]{:S(2)}) %collective-permute-start.4) | collective-permute-done | bytes 524320 | tf_op jit(solution)/shard_map/ppermute | solution.py:10
  79.0 0.8 collective-permute-start.7
  79.8 1.5 %collective-permute-start.5 = (bf16[2,128,512]{2,1,0:T(8,128)(2,1)S(1)}, bf16[2,128,512]{2,1,0:T(8,128)(2,1)S(1)}, u32[]{:S(2)}, u32[]{:S(2)}) collective-permute-start(bf16[2,128,512]{2,1,0:T(8,128)(2,1)S(1)} %get-tuple-element.24), channel_id=1, source_target_pairs={{0,2},{2,0},{4,6},{6,4},{8,10},{10,8},{12,14},{14,12},{1,3},{3,1},... | collective-permute-start | bytes 786440 | tf_op jit(solution)/shard_map/ppermute | solution.py:10
  81.3 5.4 %collective-permute-done.7 = bf16[2,128,512]{2,1,0:T(8,128)(2,1)S(1)} collective-permute-done((bf16[2,128,512]{2,1,0:T(8,128)(2,1)S(1)}, bf16[2,128,512]{2,1,0:T(8,128)(2,1)S(1)}, u32[]{:S(2)}, u32[]{:S(2)}) %collective-permute-start.7) | collective-permute-done | bytes 262176 | tf_op jit(solution)/shard_map/ppermute | solution.py:10
  86.7 1.5 %collective-permute-start.8 = (bf16[2,2,128,512]{3,2,1,0:T(8,128)(2,1)S(1)}, bf16[2,2,128,512]{3,2,1,0:T(8,128)(2,1)S(1)}, u32[]{:S(2)}, u32[]{:S(2)}) collective-permute-start(bf16[2,2,128,512]{3,2,1,0:T(8,128)(2,1)S(1)} %pad_maximum_fusion.7), channel_id=1, source_target_pairs={{0,2},{2,0},{4,6},{6,4},{8,10},{10,8},{12,14},{14,12},{1,3},{3,1},... | collective-permute-start | bytes 1572872 | tf_op jit(solution)/shard_map/ppermute | solution.py:10
  88.3 1.5 %collective-permute-start.6 = (bf16[2,2,128,512]{3,2,1,0:T(8,128)(2,1)S(1)}, bf16[2,2,128,512]{3,2,1,0:T(8,128)(2,1)S(1)}, u32[]{:S(2)}, u32[]{:S(2)}) collective-permute-start(bf16[2,2,128,512]{3,2,1,0:T(8,128)(2,1)S(1)} %pad_maximum_fusion.6), channel_id=1, source_target_pairs={{0,4},{2,6},{4,0},{6,2},{8,12},{10,14},{12,8},{14,10},{1,5},{3,7},... | collective-permute-start | bytes 1572872 | tf_op jit(solution)/shard_map/ppermute | solution.py:10
  89.8 9.4 %collective-permute-done.8 = bf16[2,2,128,512]{3,2,1,0:T(8,128)(2,1)S(1)} collective-permute-done((bf16[2,2,128,512]{3,2,1,0:T(8,128)(2,1)S(1)}, bf16[2,2,128,512]{3,2,1,0:T(8,128)(2,1)S(1)}, u32[]{:S(2)}, u32[]{:S(2)}) %collective-permute-start.8) | collective-permute-done | bytes 524320 | tf_op jit(solution)/shard_map/ppermute | solution.py:10
  99.2 1.6 %collective-permute-done.6 = bf16[2,2,128,512]{3,2,1,0:T(8,128)(2,1)S(1)} collective-permute-done((bf16[2,2,128,512]{3,2,1,0:T(8,128)(2,1)S(1)}, bf16[2,2,128,512]{3,2,1,0:T(8,128)(2,1)S(1)}, u32[]{:S(2)}, u32[]{:S(2)}) %collective-permute-start.6) | collective-permute-done | bytes 524320 | tf_op jit(solution)/shard_map/ppermute | solution.py:10
  100.8 1.4 %maximum_maximum_fusion = bf16[4,2,256,512]{3,2,1,0:T(8,128)(2,1)} fusion(bf16[1,2,128,512]{3,2,1,0:T(8,128)(2,1)S(1)} %get-tuple-element.26, bf16[1,2,128,512]{3,2,1,0:T(8,128)(2,1)S(1)} %bitcast.163, bf16[1,2,128,512]{3,2,1,0:T(8,128)(2,1)S(1)} %get-tuple-element.25, bf16[1,2,128,512]{3,2,1,0:T(8,128)(2,1)S(1)} %get-tuple-element.22, ...), kind=kLoop, calls=%fused_computation.12 | loop fusion | flops 14680064 | bytes 4194304 | tf_op jit(solution)/shard_map/concatenate | solution.py:83
  102.1 1.7 %convert_element_type.28 = bf16[2,512,512]{2,1,0:T(8,128)(2,1)S(1)} convert(f32[2,512,512]{2,1,0:T(8,128)} %param.4) | non-fusion elementwise | flops 524288 | bytes 3145728 | tf_op jit(solution)/shard_map/convert_element_type | solution.py:86
  103.9 2.8 %collective-permute-done.9 = bf16[4,2,256,512]{3,2,1,0:T(8,128)(2,1)} collective-permute-done((bf16[4,2,256,512]{3,2,1,0:T(8,128)(2,1)}, bf16[4,2,256,512]{3,2,1,0:T(8,128)(2,1)}, u32[]{:S(2)}, u32[]{:S(2)}) %collective-permute-start.9) | collective-permute-done | bytes 2097184 | tf_op jit(solution)/shard_map/ppermute | solution.py:10
  106.6 2.0 %broadcast_select_fusion = (bf16[4,2,256,512]{3,2,1,0:T(8,128)(2,1)S(1)}, bf16[4,2,256,512]{3,2,1,0:T(8,128)(2,1)S(1)}) fusion(bf16[4,2,256,512]{3,2,1,0:T(8,128)(2,1)} %collective-permute-done.9, pred[]{:T(512)S(6)} %eq.17, bf16[1,2,128,512]{3,2,1,0:T(8,128)(2,1)S(1)} %get-tuple-element.26, bf16[1,2,128,512]{3,2,1,0:T(8,128)(2,1)S(1)} %bitcast.164, ...), kind=kLoop, calls=%fused_computation.15 | loop fusion | flops 16777216 | bytes 8388609 | tf_op jit(solution)/shard_map/jit(_where)/select_n | solution.py:33
  111.2 1.8 %collective-permute-done.10 = bf16[2,512,256]{1,2,0:T(8,128)(2,1)S(1)} collective-permute-done((bf16[2,512,256]{1,2,0:T(8,128)(2,1)S(1)}, bf16[2,512,256]{1,2,0:T(8,128)(2,1)S(1)}, u32[]{:S(2)}, u32[]{:S(2)}) %collective-permute-start.10) | collective-permute-done | bytes 524320 | tf_op jit(solution)/shard_map/ppermute | solution.py:10
  117.3 1.8 %collective-permute-done.11 = bf16[2,512,256]{1,2,0:T(8,128)(2,1)S(1)} collective-permute-done((bf16[2,512,256]{1,2,0:T(8,128)(2,1)S(1)}, bf16[2,512,256]{1,2,0:T(8,128)(2,1)S(1)}, u32[]{:S(2)}, u32[]{:S(2)}) %collective-permute-start.11) | collective-permute-done | bytes 524320 | tf_op jit(solution)/shard_map/ppermute | solution.py:10
  121.2 1.5 %pad_maximum_fusion.1 = f32[2,512,512]{2,1,0:T(8,128)} fusion(f32[1,512,512]{2,1,0:T(8,128)S(1)} %fusion.1, f32[1,512,512]{2,1,0:T(8,128)S(1)} %fusion.2), kind=kLoop, calls=%fused_computation.13 | loop fusion | flops 524288 | bytes 4194304 | tf_op jit(solution)/shard_map/stack | solution.py:19
  (59 shorter events, 15.8 us)
Async XLA Ops:
  1.5 26.2 %collective-permute-start = (bf16[2,2,256,512]{3,2,1,0:T(8,128)(2,1)S(1)}, bf16[2,2,256,512]{3,2,1,0:T(8,128)(2,1)S(1)}, u32[]{:S(2)}, u32[]{:S(2)}) collective-permute-start(bf16[2,2,256,512]{3,2,1,0:T(8,128)(2,1)S(1)} %dynamic-slice_bitcast_fusion.1), channel_id=1, source_target_pairs={{0,2},{2,0},{4,6},{6,4},{8,10},{10,8},{12,14},{14,12},{1,3},{3,1},... | collective-permute-start | bytes 3145736 | tf_op jit(solution)/shard_map/ppermute | solution.py:10
  27.7 2.7 %collective-permute-start.1 = (bf16[2,2,256,512]{3,2,1,0:T(8,128)(2,1)S(1)}, bf16[2,2,256,512]{3,2,1,0:T(8,128)(2,1)S(1)}, u32[]{:S(2)}, u32[]{:S(2)}) collective-permute-start(bf16[2,2,256,512]{3,2,1,0:T(8,128)(2,1)S(1)} %collective-permute-done), channel_id=1, source_target_pairs={{0,1},{1,0},{2,3},{3,2},{4,5},{5,4},{6,7},{7,6},{8,9},{9,8},{10,11... | collective-permute-start | bytes 3145736 | tf_op jit(solution)/shard_map/ppermute | solution.py:10
  27.7 2.8 %copy-start = (bf16[1,4,2,512,512]{4,3,2,1,0:T(8,128)(2,1)S(1)}, bf16[1,4,2,512,512]{4,3,2,1,0:T(8,128)(2,1)}, u32[]{:S(2)}) copy-start(bf16[1,4,2,512,512]{4,3,2,1,0:T(8,128)(2,1)} %param.5) | copy-start | bytes 12582916
  34.6 14.1 %collective-permute-start.2 = (bf16[2,256,512]{2,1,0:T(8,128)(2,1)S(1)}, bf16[2,256,512]{2,1,0:T(8,128)(2,1)S(1)}, u32[]{:S(2)}, u32[]{:S(2)}) collective-permute-start(bf16[2,256,512]{2,1,0:T(8,128)(2,1)S(1)} %dynamic-slice_bitcast_fusion.2), channel_id=1, source_target_pairs={{0,4},{2,6},{4,0},{6,2},{8,12},{10,14},{12,8},{14,10},{1,5},{3,7},... | collective-permute-start | bytes 1572872 | tf_op jit(solution)/shard_map/ppermute | solution.py:10
  49.2 2.0 %collective-permute-start.3 = (bf16[2,256,512]{2,1,0:T(8,128)(2,1)S(1)}, bf16[2,256,512]{2,1,0:T(8,128)(2,1)S(1)}, u32[]{:S(2)}, u32[]{:S(2)}) collective-permute-start(bf16[2,256,512]{2,1,0:T(8,128)(2,1)S(1)} %convolution_convert_fusion), channel_id=1, source_target_pairs={{0,1},{1,0},{2,3},{3,2},{4,5},{5,4},{6,7},{7,6},{8,9},{9,8},{10,11... | collective-permute-start | bytes 1572872 | tf_op jit(solution)/shard_map/ppermute | solution.py:10
  52.2 3.2 %copy-start.1 = (s32[4]{0:T(128)S(1)}, s32[4]{0:T(128)}, u32[]{:S(2)}) copy-start(s32[4]{0:T(128)} %param.6) | copy-start | bytes 52
  52.5 26.3 %collective-permute-start.4 = (bf16[2,256,512]{2,1,0:T(8,128)(2,1)S(1)}, bf16[2,256,512]{2,1,0:T(8,128)(2,1)S(1)}, u32[]{:S(2)}, u32[]{:S(2)}) collective-permute-start(bf16[2,256,512]{2,1,0:T(8,128)(2,1)S(1)} %pad_maximum_fusion.5), channel_id=1, source_target_pairs={{0,8},{2,10},{4,12},{6,14},{8,0},{10,2},{12,4},{14,6},{1,9},{3,11}... | collective-permute-start | bytes 1572872 | tf_op jit(solution)/shard_map/ppermute | solution.py:10
  79.0 7.7 %collective-permute-start.7 = (bf16[2,128,512]{2,1,0:T(8,128)(2,1)S(1)}, bf16[2,128,512]{2,1,0:T(8,128)(2,1)S(1)}, u32[]{:S(2)}, u32[]{:S(2)}) collective-permute-start(bf16[2,128,512]{2,1,0:T(8,128)(2,1)S(1)} %get-tuple-element.23), channel_id=1, source_target_pairs={{0,4},{2,6},{4,0},{6,2},{8,12},{10,14},{12,8},{14,10},{1,5},{3,7},... | collective-permute-start | bytes 786440 | tf_op jit(solution)/shard_map/ppermute | solution.py:10
  79.8 8.5 %collective-permute-start.5 = (bf16[2,128,512]{2,1,0:T(8,128)(2,1)S(1)}, bf16[2,128,512]{2,1,0:T(8,128)(2,1)S(1)}, u32[]{:S(2)}, u32[]{:S(2)}) collective-permute-start(bf16[2,128,512]{2,1,0:T(8,128)(2,1)S(1)} %get-tuple-element.24), channel_id=1, source_target_pairs={{0,2},{2,0},{4,6},{6,4},{8,10},{10,8},{12,14},{14,12},{1,3},{3,1},... | collective-permute-start | bytes 786440 | tf_op jit(solution)/shard_map/ppermute | solution.py:10
  86.7 12.4 %collective-permute-start.8 = (bf16[2,2,128,512]{3,2,1,0:T(8,128)(2,1)S(1)}, bf16[2,2,128,512]{3,2,1,0:T(8,128)(2,1)S(1)}, u32[]{:S(2)}, u32[]{:S(2)}) collective-permute-start(bf16[2,2,128,512]{3,2,1,0:T(8,128)(2,1)S(1)} %pad_maximum_fusion.7), channel_id=1, source_target_pairs={{0,2},{2,0},{4,6},{6,4},{8,10},{10,8},{12,14},{14,12},{1,3},{3,1},... | collective-permute-start | bytes 1572872 | tf_op jit(solution)/shard_map/ppermute | solution.py:10
  88.3 12.5 %collective-permute-start.6 = (bf16[2,2,128,512]{3,2,1,0:T(8,128)(2,1)S(1)}, bf16[2,2,128,512]{3,2,1,0:T(8,128)(2,1)S(1)}, u32[]{:S(2)}, u32[]{:S(2)}) collective-permute-start(bf16[2,2,128,512]{3,2,1,0:T(8,128)(2,1)S(1)} %pad_maximum_fusion.6), channel_id=1, source_target_pairs={{0,4},{2,6},{4,0},{6,2},{8,12},{10,14},{12,8},{14,10},{1,5},{3,7},... | collective-permute-start | bytes 1572872 | tf_op jit(solution)/shard_map/ppermute | solution.py:10
  102.1 4.5 %collective-permute-start.9 = (bf16[4,2,256,512]{3,2,1,0:T(8,128)(2,1)}, bf16[4,2,256,512]{3,2,1,0:T(8,128)(2,1)}, u32[]{:S(2)}, u32[]{:S(2)}) collective-permute-start(bf16[4,2,256,512]{3,2,1,0:T(8,128)(2,1)} %maximum_maximum_fusion), channel_id=1, source_target_pairs={{0,1},{1,0},{2,3},{3,2},{4,5},{5,4},{6,7},{7,6},{8,9},{9,8},{10,11... | collective-permute-start | bytes 6291464 | tf_op jit(solution)/shard_map/ppermute | solution.py:10
  111.0 2.0 %collective-permute-start.10 = (bf16[2,512,256]{1,2,0:T(8,128)(2,1)S(1)}, bf16[2,512,256]{1,2,0:T(8,128)(2,1)S(1)}, u32[]{:S(2)}, u32[]{:S(2)}) collective-permute-start(bf16[2,512,256]{1,2,0:T(8,128)(2,1)S(1)} %fusion.41), channel_id=1, source_target_pairs={{0,1},{1,0},{2,3},{3,2},{4,5},{5,4},{6,7},{7,6},{8,9},{9,8},{10,11... | collective-permute-start | bytes 1572872 | tf_op jit(solution)/shard_map/ppermute | solution.py:10
  117.1 2.0 %collective-permute-start.11 = (bf16[2,512,256]{1,2,0:T(8,128)(2,1)S(1)}, bf16[2,512,256]{1,2,0:T(8,128)(2,1)S(1)}, u32[]{:S(2)}, u32[]{:S(2)}) collective-permute-start(bf16[2,512,256]{1,2,0:T(8,128)(2,1)S(1)} %fusion.39), channel_id=1, source_target_pairs={{0,1},{1,0},{2,3},{3,2},{4,5},{5,4},{6,7},{7,6},{8,9},{9,8},{10,11... | collective-permute-start | bytes 1572872 | tf_op jit(solution)/shard_map/ppermute | solution.py:10

commit v2 on v0

v2 whole, which is shorter than its diff:
```python
import functools

import jax
import jax.numpy as jnp
from jax import lax
from jax.experimental import pallas as pl
from jax.experimental.pallas import tpu as pltpu
from jax.sharding import PartitionSpec as P

GROUP = 4
CHUNKS = 4
TILE = 128
BF16 = jnp.bfloat16
F32 = jnp.float32


def dot(x, y):
    return jnp.dot(x, y, preferred_element_type=F32)


def complex_product(ar, ai, br, bi):
    return dot(ar, br) - dot(ai, bi), dot(ar, bi) + dot(ai, br)


def remote(src, dst, send_sem, recv_sem, device):
    return pltpu.make_async_remote_copy(
        src_ref=src,
        dst_ref=dst,
        send_sem=send_sem,
        recv_sem=recv_sem,
        device_id=device,
        device_id_type=pl.DeviceIdType.MESH,
    )


def kernel(
    rounds, roots, orders, stem_in, leaves_in, out,
    leaf, pair, away, high, chosen, held, crossed, branches, stem, net1, net2, net3, swap,
    local_sem, leaf_s, leaf_r, fwd_s, fwd_r, pair_s, pair_r, high_s, high_r,
    cross_s, cross_r, z_s, z_r, y_s, y_r, core_s, core_r, swap_s, swap_r,
):
    width = stem.shape[2]
    rows = stem.shape[1]
    half = width // 2
    part = half // CHUNKS
    core = lax.axis_index("narrow")
    wide = lax.axis_index("wide")
    member = wide % GROUP
    y = member % 2
    z = member // 2
    other = {"narrow": 1 - core}
    over_y = {"wide": wide + 1 - 2 * y}
    over_z = {"wide": wide + 2 - 4 * z}
    bits = [(wide // (GROUP << r)) % 2 for r in range(rounds)]
    over_group = [{"wide": wide + (GROUP << r) * (1 - 2 * bits[r])} for r in range(rounds)]

    barrier = pltpu.get_barrier_semaphore()
    for peer in [other, over_y, over_z] + over_group:
        pl.semaphore_signal(barrier, inc=1, device_id=peer, device_id_type=pl.DeviceIdType.MESH)
    own_rows = pl.ds(pl.multiple_of(core * half, half), half)
    own_copies = [
        pltpu.make_async_copy(leaves_in.at[0, 2 * s + y], leaf.at[s, y], local_sem.at[s])
        for s in range(2)
    ]
    stem_copy = pltpu.make_async_copy(stem_in, stem, local_sem.at[2])
    pl.semaphore_wait(barrier, 3 + rounds)

    phases = [1 - z, z]
    leaf_copies = []
    for i, s in enumerate(phases):
        copy = remote(
            leaves_in.at[0, 2 * s + 1 - y, :, own_rows],
            leaf.at[s, y, :, own_rows],
            leaf_s.at[i], leaf_r.at[i], over_y,
        )
        copy.start()
        leaf_copies.append(copy)
    for copy in own_copies:
        copy.start()
    stem_copy.start()

    def choose(i, carry):
        column = lax.broadcasted_iota(jnp.int32, (TILE, width), 1)
        source = jnp.zeros((TILE, width), jnp.int32)
        for b in range(orders.shape[1]):
            weight = jnp.left_shift(jnp.int32(1), orders[member, b])
            source = source + (jnp.right_shift(column, b) & 1) * weight
        row = lax.broadcasted_iota(jnp.int32, (TILE, width), 0) + i * TILE
        at = pl.ds(pl.multiple_of(i * TILE, TILE), TILE)
        chosen[at] = jnp.where(row == source, 1.0, 0.0).astype(F32).astype(BF16)
        return carry

    lax.fori_loop(0, width // TILE, choose, 0)
    for copy in own_copies:
        copy.wait()

    pair_copy = remote(away, pair.at[z], pair_s, pair_r, over_z)
    for i, s in enumerate(phases):
        leaf_copies[i].wait_recv()
        forward = remote(
            leaf.at[s, 1 - y, :, own_rows], leaf.at[s, 1 - y, :, own_rows],
            fwd_s.at[i], fwd_r.at[i], other,
        )
        forward.start()
        forward.wait()

        def pair_tile(t, carry, s=s, i=i):
            source = pl.ds(pl.multiple_of(core * half + t * TILE, TILE), TILE)
            at = pl.ds(pl.multiple_of(t * TILE, TILE), TILE)
            real, imag = complex_product(
                leaf[s, 0, 0, source], leaf[s, 0, 1, source], leaf[s, 1, 0], leaf[s, 1, 1]
            )
            target = away if i == 0 else pair.at[z]
            target[0, at] = real.astype(BF16)
            target[1, at] = imag.astype(BF16)
            return carry

        lax.fori_loop(0, half // TILE, pair_tile, 0)
        if i == 0:
            pair_copy.start()
    pair_copy.wait_recv()

    def high_tile(t, carry):
        source = pl.ds(pl.multiple_of(t * TILE, TILE), TILE)
        at = pl.ds(pl.multiple_of(core * half + t * TILE, TILE), TILE)
        for c in range(2):
            high[c, at] = dot(pair[1, c, source], chosen[...]).astype(BF16)
        return carry

    lax.fori_loop(0, half // TILE, high_tile, 0)
    high_copy = remote(high.at[:, own_rows], high.at[:, own_rows], high_s, high_r, other)
    high_copy.start()
    high_copy.wait()

    def rows_of(c):
        return pl.ds(pl.multiple_of(core * half + c * part, part), part)

    def cross_copy(r, c):
        return remote(held.at[r, c], crossed.at[r, c], cross_s.at[r, c], cross_r.at[r, c], over_group[r])

    def place(origin, c):
        return branches.at[origin, :, rows_of(c)]

    origins = [member, member + 2 - 4 * z, member + 1 - 2 * y, GROUP - 1 - member]

    def z_copy(c):
        return remote(place(origins[0], c), place(origins[0], c), z_s.at[c], z_r.at[c], over_z)

    def y_copy(i, c):
        return remote(place(origins[i], c), place(origins[i], c), y_s.at[i, c], y_r.at[i, c], over_y)

    def core_copy(i, c):
        return remote(place(origins[i], c), place(origins[i], c), core_s.at[i, c], core_r.at[i, c], other)

    for c in range(CHUNKS):
        at = pl.ds(c * part, part)
        real, imag = complex_product(pair[0, 0, at], pair[0, 1, at], high[0], high[1])
        if rounds:
            held[0, c, 0] = real.astype(BF16)
            held[0, c, 1] = imag.astype(BF16)
            cross_copy(0, c).start()
        else:
            branches[member, 0, rows_of(c)] = real.astype(BF16)
            branches[member, 1, rows_of(c)] = imag.astype(BF16)

    for r in range(rounds):
        root_bit = (roots[member] // (GROUP << r)) % 2
        for c in range(CHUNKS):
            cross_copy(r, c).wait_recv()
            for p in range(2):
                here = held[r, c, p].astype(F32)
                there = crossed[r, c, p].astype(F32)
                same = jnp.full(here.shape, root_bit, jnp.int32) == bits[r]
                picked = jnp.where(same, here, there).astype(BF16)
                if r + 1 < rounds:
                    held[r + 1, c, p] = picked
                else:
                    branches[member, p, rows_of(c)] = picked
            if r + 1 < rounds:
                cross_copy(r + 1, c).start()
            else:
                z_copy(c).start()
                y_copy(0, c).start()
                core_copy(0, c).start()
                if c > 0:
                    z_copy(c - 1).wait_recv()
                    y_copy(1, c - 1).start()
                    core_copy(1, c - 1).start()
                    y_copy(0, c - 1).wait_recv()
                    core_copy(2, c - 1).start()
                if c > 1:
                    y_copy(1, c - 2).wait_recv()
                    core_copy(3, c - 2).start()
    if not rounds:
        for c in range(CHUNKS):
            z_copy(c).start()
            y_copy(0, c).start()
            core_copy(0, c).start()
    for c in range(0 if not rounds else CHUNKS - 1, CHUNKS):
        z_copy(c).wait_recv()
        y_copy(1, c).start()
        core_copy(1, c).start()
        y_copy(0, c).wait_recv()
        core_copy(2, c).start()
    for c in range(0 if not rounds else CHUNKS - 2, CHUNKS):
        y_copy(1, c).wait_recv()
        core_copy(3, c).start()
    stem_copy.wait()
    for c in range(CHUNKS):
        for i in range(4):
            core_copy(i, c).wait_recv()

    def columns(block):
        return pl.ds(pl.multiple_of(block * half, half), half)

    def swapped(step, index, read, target):
        copy = remote(swap.at[index], target.at[core], swap_s.at[index], swap_r.at[index], other)
        for keep in range(2):
            block = core if keep else 1 - core

            def tile(t, carry, keep=keep, block=block):
                at = pl.ds(pl.multiple_of(t * TILE, TILE), TILE)
                nr, ni = read(at)
                real, imag = complex_product(
                    nr, ni, branches[step, 0, :, columns(block)], branches[step, 1, :, columns(block)]
                )
                place = target.at[core] if keep else swap.at[index]
                place[0, at] = real.astype(BF16)
                place[1, at] = imag.astype(BF16)
                return carry

            lax.fori_loop(0, rows // TILE, tile, 0)
            if not keep:
                copy.start()
        copy.wait()

    def plain(step, source, target):
        def tile(t, carry):
            at = pl.ds(pl.multiple_of(t * TILE, TILE), TILE)
            real = jnp.zeros((TILE, width), F32)
            imag = jnp.zeros((TILE, width), F32)
            for block in range(2):
                inner = pl.ds(block * half, half)
                dr, di = complex_product(
                    source[block, 0, at], source[block, 1, at],
                    branches[step, 0, inner], branches[step, 1, inner],
                )
                real, imag = real + dr, imag + di
            target[0, at] = real.astype(target.dtype)
            target[1, at] = imag.astype(target.dtype)
            return carry

        lax.fori_loop(0, rows // TILE, tile, 0)

    swapped(0, 0, lambda at: (stem[0, at].astype(BF16), stem[1, at].astype(BF16)), net1)
    plain(1, net1, net2)
    swapped(2, 1, lambda at: (net2[0, at], net2[1, at]), net3)
    plain(3, net3, out)

    for copy in leaf_copies:
        copy.wait_send()
    pair_copy.wait_send()
    for c in range(CHUNKS):
        for r in range(rounds):
            cross_copy(r, c).wait_send()
        z_copy(c).wait_send()
        for i in range(2):
            y_copy(i, c).wait_send()
        for i in range(4):
            core_copy(i, c).wait_send()


def local(stem_tensor, leaves, root_devices, mode_orders):
    _, rows, width = stem_tensor.shape
    half = width // 2
    part = half // CHUNKS
    groups = lax.axis_size("wide") // GROUP
    rounds = groups.bit_length() - 1
    vmem = pltpu.VMEM
    dma = pltpu.SemaphoreType.DMA
    return pl.pallas_call(
        functools.partial(kernel, rounds),
        out_shape=jax.ShapeDtypeStruct(stem_tensor.shape, F32),
        in_specs=[pl.BlockSpec(memory_space=pltpu.SMEM)] * 2
        + [pl.BlockSpec(memory_space=pl.ANY)] * 2,
        out_specs=pl.BlockSpec(memory_space=pltpu.VMEM),
        scratch_shapes=[
            vmem((2, 2, 2, width, width), BF16),
            vmem((2, 2, half, width), BF16),
            vmem((2, half, width), BF16),
            vmem((2, width, width), BF16),
            vmem((width, width), BF16),
            vmem((max(rounds, 1), CHUNKS, 2, part, width), BF16),
            vmem((max(rounds, 1), CHUNKS, 2, part, width), BF16),
            vmem((GROUP, 2, width, width), BF16),
            vmem((2, rows, width), F32),
            vmem((2, 2, rows, half), BF16),
            vmem((2, rows, width), BF16),
            vmem((2, 2, rows, half), BF16),
            vmem((2, 2, rows, half), BF16),
            dma((3,)),
            dma((2,)), dma((2,)), dma((2,)), dma((2,)),
            dma, dma, dma, dma,
            dma((max(rounds, 1), CHUNKS)), dma((max(rounds, 1), CHUNKS)),
            dma((CHUNKS,)), dma((CHUNKS,)),
            dma((2, CHUNKS)), dma((2, CHUNKS)),
            dma((4, CHUNKS)), dma((4, CHUNKS)),
            dma((2,)), dma((2,)),
        ],
        compiler_params=pltpu.CompilerParams(collective_id=0, has_side_effects=True),
    )(root_devices, mode_orders, stem_tensor, leaves)


def solution(mesh):
    stem_spec = P(None, ("cuts", "wide", "narrow"), None)
    return jax.shard_map(
        local,
        mesh=mesh,
        in_specs=(stem_spec, P(("cuts", "wide"), None, None, None, None), P(), P()),
        out_specs=stem_spec,
        check_vma=False,
    )
```

time: 476 us -> 94.9 us (0.20); the launches traced: 471 us -> 94.7 us
  waiting for transfers between devices: 283 us -> 0 us
  Pallas kernels: 0 us -> 91.6 us
  matrix products: 65.1 us -> 0 us
  local copies, waits for them, and re-layouts: 47.5 us -> 3.08 us
  other arithmetic: 36.5 us -> 0 us
  starting transfers between devices: 21.4 us -> 0 us
  between operations: 16.7 us -> 0.01 us
    psum x1 -> x0, waiting for transfers between devices: 156 us -> none  [broadcast(): return lax.psum(block, axis)]
    ppermute x8 -> x0, waiting for transfers between devices: 116 us -> none  [from_partner(): lax.ppermute(value, axis, [(i, i ^ 1 << apart) for i in range(lax.axis_si...]
    pallas_call x0 -> x1, Pallas kernels: none -> 91.6 us  [local(): pl.pallas_call(functools.partial(kernel, rounds), out_shape=jax.ShapeDtyp...]
    dot_general x48 -> x0, matrix products: 65.1 us -> none  [the longest x12 17.9 us: complex_product(): jnp.dot(left_matrix[1], right_matrix[0], preferred_element_type=jnp.float...]
    select_n x17 -> x0, other arithmetic: 26.4 us -> none  [the longest x4 11.5 us: broadcast(): jnp.where(lax.axis_index(axis) == holder, block, jnp.zeros_like(block))]
    slice x7 -> x0, local copies, waits for them, and re-layouts: 21.5 us -> none  [the longest x3 12.1 us: complex_product(): right_matrix[0]]
    gather x4 -> x0, local copies, waits for them, and re-layouts: 11.9 us -> none  [local(): ordered_part = jnp.take(branch_part, source, axis=2)]
    ppermute x8 -> x0, starting transfers between devices: 10.5 us -> none  [from_partner(): lax.ppermute(value, axis, [(i, i ^ 1 << apart) for i in range(lax.axis_si...]
  transfers between devices with their start and end apart: 19 -> 0, of which waited for: 7 -> 0; matrix products, arithmetic and copies ran while one was open for 18% -> 0% of each run, Pallas kernels for 0% -> 0%
where the time goes in v2:
time: 94.9 us; the launch traced here: 94.7 us
  Pallas kernels  91.6 us (97%)
  local copies, waits for them, and re-layouts  3.08 us (3%)
    pallas_call x1, Pallas kernels, local(): pl.pallas_call(functools.partial(kernel, rounds), out_shape=jax.ShapeDtyp...  91.6 us
    unnamed x1, local copies, waits for them, and re-layouts  3.08 us

profile of v2, /device:TPU:0, one launch (start us, length us, event | category | flops | bytes accessed | tf_op | source)
XLA Modules:
  0.0 94.7 jit_solution(14729753671952736758)
XLA Ops:
  0.0 91.6 %shard_map.46 = f32[2,512,512]{2,1,0:T(8,128)} custom-call(s32[4]{0:T(128)} %roots.1, s32[4,9]{1,0:T(4,128)} %orders.1, f32[2,512,512]{2,1,0:T(8,128)} %stem_in.1, bf16[1,4,2,512,512]{4,3,2,1,0:T(8,128)(2,1)} %leaves_in.1), custom_call_target="tpu_custom_call" | custom-call | tf_op jit(solution)/shard_map/pallas_call | solution.py:281
  91.6 3.1 %copy.6 = f32[2,512,512]{2,1,0:T(8,128)} copy(f32[2,512,512]{2,1,0:T(8,128)} %shard_map.46) | data formatting | bytes 4194304

commit v3 on v2

--- a/solution.py
+++ b/solution.py
@@ -8,7 +8,8 @@
 from jax.sharding import PartitionSpec as P
 
 GROUP = 4
-CHUNKS = 4
+CHUNKS = 8
+FLIGHT = 2
 TILE = 128
 BF16 = jnp.bfloat16
 F32 = jnp.float32
@@ -19,7 +20,11 @@
 
 
 def complex_product(ar, ai, br, bi):
-    return dot(ar, br) - dot(ai, bi), dot(ar, bi) + dot(ai, br)
+    left = jnp.concatenate([ar, ai], axis=1)
+    return (
+        dot(left, jnp.concatenate([br, -bi], axis=0)),
+        dot(left, jnp.concatenate([bi, br], axis=0)),
+    )
 
 
 def remote(src, dst, send_sem, recv_sem, device):
@@ -34,7 +39,7 @@
 
 
 def kernel(
-    rounds, roots, orders, stem_in, leaves_in, out,
+    rounds, roots, orders, stem_in, leaves_in, net_out, last_out,
     leaf, pair, away, high, chosen, held, crossed, branches, stem, net1, net2, net3, swap,
     local_sem, leaf_s, leaf_r, fwd_s, fwd_r, pair_s, pair_r, high_s, high_r,
     cross_s, cross_r, z_s, z_r, y_s, y_r, core_s, core_r, swap_s, swap_r,
@@ -73,8 +78,8 @@
             leaf.at[s, y, :, own_rows],
             leaf_s.at[i], leaf_r.at[i], over_y,
         )
-        copy.start()
         leaf_copies.append(copy)
+    leaf_copies[0].start()
     for copy in own_copies:
         copy.start()
     stem_copy.start()
@@ -95,6 +100,8 @@
         copy.wait()
 
     pair_copy = remote(away, pair.at[z], pair_s, pair_r, over_z)
+    leaf_copies[0].wait_send()
+    leaf_copies[1].start()
     for i, s in enumerate(phases):
         leaf_copies[i].wait_recv()
         forward = remote(
@@ -105,29 +112,28 @@
         forward.wait()
 
         def pair_tile(t, carry, s=s, i=i):
-            source = pl.ds(pl.multiple_of(core * half + t * TILE, TILE), TILE)
-            at = pl.ds(pl.multiple_of(t * TILE, TILE), TILE)
+            at = pl.ds(pl.multiple_of(t * half, half), half)
             real, imag = complex_product(
-                leaf[s, 0, 0, source], leaf[s, 0, 1, source], leaf[s, 1, 0], leaf[s, 1, 1]
+                leaf[s, 0, 0, own_rows], leaf[s, 0, 1, own_rows],
+                leaf[s, 1, 0, :, at], leaf[s, 1, 1, :, at],
             )
             target = away if i == 0 else pair.at[z]
-            target[0, at] = real.astype(BF16)
-            target[1, at] = imag.astype(BF16)
+            target[0, :, at] = real.astype(BF16)
+            target[1, :, at] = imag.astype(BF16)
             return carry
 
-        lax.fori_loop(0, half // TILE, pair_tile, 0)
+        lax.fori_loop(0, width // half, pair_tile, 0)
         if i == 0:
             pair_copy.start()
     pair_copy.wait_recv()
 
     def high_tile(t, carry):
-        source = pl.ds(pl.multiple_of(t * TILE, TILE), TILE)
-        at = pl.ds(pl.multiple_of(core * half + t * TILE, TILE), TILE)
+        at = pl.ds(pl.multiple_of(t * half, half), half)
         for c in range(2):
-            high[c, at] = dot(pair[1, c, source], chosen[...]).astype(BF16)
+            high[c, own_rows, at] = dot(pair[1, c], chosen[:, at]).astype(BF16)
         return carry
 
-    lax.fori_loop(0, half // TILE, high_tile, 0)
+    lax.fori_loop(0, width // half, high_tile, 0)
     high_copy = remote(high.at[:, own_rows], high.at[:, own_rows], high_s, high_r, other)
     high_copy.start()
     high_copy.wait()
@@ -151,6 +157,41 @@
 
     def core_copy(i, c):
         return remote(place(origins[i], c), place(origins[i], c), core_s.at[i, c], core_r.at[i, c], other)
+
+    def spread(c):
+        z_copy(c).start()
+        y_copy(0, c).start()
+        core_copy(0, c).start()
+
+    def select(r, c):
+        cross_copy(r, c).wait_recv()
+        cross_copy(r, c).wait_send()
+        if c + FLIGHT < CHUNKS:
+            cross_copy(r, c + FLIGHT).start()
+        root_bit = (roots[member] // (GROUP << r)) % 2
+        for p in range(2):
+            here = held[r, c, p].astype(F32)
+            there = crossed[r, c, p].astype(F32)
+            same = jnp.full(here.shape, root_bit, jnp.int32) == bits[r]
+            picked = jnp.where(same, here, there).astype(BF16)
+            if r + 1 < rounds:
+                held[r + 1, c, p] = picked
+            else:
+                branches[member, p, rows_of(c)] = picked
+        if r + 1 < rounds:
+            if c < FLIGHT:
+                cross_copy(r + 1, c).start()
+        else:
+            spread(c)
+
+    def on_z(c):
+        z_copy(c).wait_recv()
+        y_copy(1, c).start()
+        core_copy(1, c).start()
+
+    def on_y(i, c):
+        y_copy(i, c).wait_recv()
+        core_copy(2 + i, c).start()
 
     for c in range(CHUNKS):
         at = pl.ds(c * part, part)
@@ -158,57 +199,30 @@
         if rounds:
             held[0, c, 0] = real.astype(BF16)
             held[0, c, 1] = imag.astype(BF16)
-            cross_copy(0, c).start()
+            if c < FLIGHT:
+                cross_copy(0, c).start()
         else:
             branches[member, 0, rows_of(c)] = real.astype(BF16)
             branches[member, 1, rows_of(c)] = imag.astype(BF16)
-
-    for r in range(rounds):
-        root_bit = (roots[member] // (GROUP << r)) % 2
+            spread(c)
+
+    for r in range(rounds - 1):
         for c in range(CHUNKS):
-            cross_copy(r, c).wait_recv()
-            for p in range(2):
-                here = held[r, c, p].astype(F32)
-                there = crossed[r, c, p].astype(F32)
-                same = jnp.full(here.shape, root_bit, jnp.int32) == bits[r]
-                picked = jnp.where(same, here, there).astype(BF16)
-                if r + 1 < rounds:
-                    held[r + 1, c, p] = picked
-                else:
-                    branches[member, p, rows_of(c)] = picked
-            if r + 1 < rounds:
-                cross_copy(r + 1, c).start()
-            else:
-                z_copy(c).start()
-                y_copy(0, c).start()
-                core_copy(0, c).start()
-                if c > 0:
-                    z_copy(c - 1).wait_recv()
-                    y_copy(1, c - 1).start()
-                    core_copy(1, c - 1).start()
-                    y_copy(0, c - 1).wait_recv()
-                    core_copy(2, c - 1).start()
-                if c > 1:
-                    y_copy(1, c - 2).wait_recv()
-                    core_copy(3, c - 2).start()
-    if not rounds:
-        for c in range(CHUNKS):
-            z_copy(c).start()
-            y_copy(0, c).start()
-            core_copy(0, c).start()
-    for c in range(0 if not rounds else CHUNKS - 1, CHUNKS):
-        z_copy(c).wait_recv()
-        y_copy(1, c).start()
-        core_copy(1, c).start()
-        y_copy(0, c).wait_recv()
-        core_copy(2, c).start()
-    for c in range(0 if not rounds else CHUNKS - 2, CHUNKS):
-        y_copy(1, c).wait_recv()
-        core_copy(3, c).start()
+            select(r, c)
+    for c in range(CHUNKS + 2):
+        if rounds and c < CHUNKS:
+            select(rounds - 1, c)
+        if 1 <= c <= CHUNKS:
+            on_z(c - 1)
+            on_y(0, c - 1)
+        if c >= 2:
+            on_y(1, c - 2)
     stem_copy.wait()
     for c in range(CHUNKS):
         for i in range(4):
             core_copy(i, c).wait_recv()
+    last_copy = pltpu.make_async_copy(branches.at[GROUP - 1], last_out, local_sem.at[3])
+    last_copy.start()
 
     def columns(block):
         return pl.ds(pl.multiple_of(block * half, half), half)
@@ -219,7 +233,7 @@
             block = core if keep else 1 - core
 
             def tile(t, carry, keep=keep, block=block):
-                at = pl.ds(pl.multiple_of(t * TILE, TILE), TILE)
+                at = pl.ds(pl.multiple_of(t * half, half), half)
                 nr, ni = read(at)
                 real, imag = complex_product(
                     nr, ni, branches[step, 0, :, columns(block)], branches[step, 1, :, columns(block)]
@@ -229,45 +243,57 @@
                 place[1, at] = imag.astype(BF16)
                 return carry
 
-            lax.fori_loop(0, rows // TILE, tile, 0)
+            lax.fori_loop(0, rows // half, tile, 0)
             if not keep:
                 copy.start()
         copy.wait()
 
     def plain(step, source, target):
-        def tile(t, carry):
-            at = pl.ds(pl.multiple_of(t * TILE, TILE), TILE)
-            real = jnp.zeros((TILE, width), F32)
-            imag = jnp.zeros((TILE, width), F32)
-            for block in range(2):
-                inner = pl.ds(block * half, half)
-                dr, di = complex_product(
-                    source[block, 0, at], source[block, 1, at],
-                    branches[step, 0, inner], branches[step, 1, inner],
+        for block in range(width // half):
+            across = pl.ds(block * half, half)
+
+            def tile(t, carry, across=across):
+                at = pl.ds(pl.multiple_of(t * half, half), half)
+                real, imag = complex_product(
+                    jnp.concatenate([source[0, 0, at], source[1, 0, at]], axis=1),
+                    jnp.concatenate([source[0, 1, at], source[1, 1, at]], axis=1),
+                    branches[step, 0, :, across], branches[step, 1, :, across],
                 )
-                real, imag = real + dr, imag + di
-            target[0, at] = real.astype(target.dtype)
-            target[1, at] = imag.astype(target.dtype)
-            return carry
-
-        lax.fori_loop(0, rows // TILE, tile, 0)
+                target[0, at, across] = real.astype(target.dtype)
+                target[1, at, across] = imag.astype(target.dtype)
+                return carry
+
+            lax.fori_loop(0, rows // half, tile, 0)
 
     swapped(0, 0, lambda at: (stem[0, at].astype(BF16), stem[1, at].astype(BF16)), net1)
     plain(1, net1, net2)
     swapped(2, 1, lambda at: (net2[0, at], net2[1, at]), net3)
-    plain(3, net3, out)
-
-    for copy in leaf_copies:
-        copy.wait_send()
+    net_copy = pltpu.make_async_copy(net3, net_out, local_sem.at[4])
+    net_copy.start()
+    net_copy.wait()
+    last_copy.wait()
+
+    leaf_copies[1].wait_send()
     pair_copy.wait_send()
     for c in range(CHUNKS):
-        for r in range(rounds):
-            cross_copy(r, c).wait_send()
         z_copy(c).wait_send()
         for i in range(2):
             y_copy(i, c).wait_send()
         for i in range(4):
             core_copy(i, c).wait_send()
+
+
+def finish(net, branch, out):
+    half = net.shape[3]
+    for block in range(branch.shape[2] // half):
+        across = pl.ds(block * half, half)
+        real, imag = complex_product(
+            jnp.concatenate([net[0, 0], net[1, 0]], axis=1),
+            jnp.concatenate([net[0, 1], net[1, 1]], axis=1),
+            branch[0, :, across], branch[1, :, across],
+        )
+        out[0, :, across] = real
+        out[1, :, across] = imag
 
 
 def local(stem_tensor, leaves, root_devices, mode_orders):
@@ -278,12 +304,15 @@
     rounds = groups.bit_length() - 1
     vmem = pltpu.VMEM
     dma = pltpu.SemaphoreType.DMA
-    return pl.pallas_call(
+    network, last = pl.pallas_call(
         functools.partial(kernel, rounds),
-        out_shape=jax.ShapeDtypeStruct(stem_tensor.shape, F32),
+        out_shape=(
+            jax.ShapeDtypeStruct((2, 2, rows, half), BF16),
+            jax.ShapeDtypeStruct((2, width, width), BF16),
+        ),
         in_specs=[pl.BlockSpec(memory_space=pltpu.SMEM)] * 2
         + [pl.BlockSpec(memory_space=pl.ANY)] * 2,
-        out_specs=pl.BlockSpec(memory_space=pltpu.VMEM),
+        out_specs=[pl.BlockSpec(memory_space=pl.ANY)] * 2,
         scratch_shapes=[
             vmem((2, 2, 2, width, width), BF16),
             vmem((2, 2, half, width), BF16),
@@ -298,7 +327,7 @@
             vmem((2, rows, width), BF16),
             vmem((2, 2, rows, half), BF16),
             vmem((2, 2, rows, half), BF16),
-            dma((3,)),
+            dma((5,)),
             dma((2,)), dma((2,)), dma((2,)), dma((2,)),
             dma, dma, dma, dma,
             dma((max(rounds, 1), CHUNKS)), dma((max(rounds, 1), CHUNKS)),
@@ -309,6 +338,16 @@
         ],
         compiler_params=pltpu.CompilerParams(collective_id=0, has_side_effects=True),
     )(root_devices, mode_orders, stem_tensor, leaves)
+    return pl.pallas_call(
+        finish,
+        grid=(rows // half,),
+        out_shape=jax.ShapeDtypeStruct(stem_tensor.shape, F32),
+        in_specs=[
+            pl.BlockSpec((2, 2, half, half), lambda i: (0, 0, i, 0)),
+            pl.BlockSpec((2, width, width), lambda i: (0, 0, 0)),
+        ],
+        out_specs=pl.BlockSpec((2, half, width), lambda i: (0, i, 0)),
+    )(network, last)
 
 
 def solution(mesh):

time: 94.9 us -> 85.7 us (0.903)
  Pallas kernels: 91.6 us -> 85.5 us
  local copies, waits for them, and re-layouts: 3.08 us -> 0 us
    pallas_call x1 -> x2, Pallas kernels: 91.6 us -> 85.5 us  [the longest x1 81.7 us: local(): pl.pallas_call(functools.partial(kernel, rounds), out_shape=(jax.ShapeDty...]
    unnamed x1 -> x0, local copies, waits for them, and re-layouts: 3.08 us -> none
where the time goes in v3:
time: 85.7 us; the launch traced here: 85.5 us
  Pallas kernels  85.5 us (100%)
    pallas_call x1, Pallas kernels, local(): pl.pallas_call(functools.partial(kernel, rounds), out_shape=(jax.ShapeDty...  81.7 us
    pallas_call x1, Pallas kernels, local(): pl.pallas_call(finish, grid=(rows // half,), out_shape=jax.ShapeDtypeStru...  3.81 us

profile of v3, /device:TPU:0, one launch (start us, length us, event | category | flops | bytes accessed | tf_op | source)
XLA Modules:
  0.0 85.5 jit_solution(12074966743353089107)
XLA Ops:
  0.0 81.7 %shard_map.46 = (bf16[2,2,512,256]{3,2,1,0:T(8,128)(2,1)}, bf16[2,512,512]{2,1,0:T(8,128)(2,1)}) custom-call(s32[4]{0:T(128)} %roots.1, s32[4,9]{1,0:T(4,128)} %orders.1, f32[2,512,512]{2,1,0:T(8,128)} %stem_in.1, bf16[1,4,2,512,512]{4,3,2,1,0:T(8,128)(2,1)} %leaves_in.1), custom_call_target="tpu_custom_call" | custom-call | tf_op jit(solution)/shard_map/pallas_call | solution.py:307
  81.7 3.8 %shard_map.47 = f32[2,512,512]{2,1,0:T(8,128)} custom-call(bf16[2,2,512,256]{3,2,1,0:T(8,128)(2,1)} %get-tuple-element.7.net, bf16[2,512,512]{2,1,0:T(8,128)(2,1)} %get-tuple-element.8.branch), custom_call_target="tpu_custom_call" | custom-call | tf_op jit(solution)/shard_map/pallas_call | solution.py:341
